TPU v7x, 32 devices: a whole 2x2x4 slice. The times are simulated.
32 devices in a mesh: dp: 16 (over z, y, x), mp: 2 (over core).
Axes of the slice: x: 2, y: 2, z: 4, core: 2. Of those that a mesh axis runs over, the one named last changes fastest.
Arguments:
- hidden_state: bfloat16 [32, 19, 19, 256], P('dp'), may hold values from -6 to 6
- actions: int32 [32, 2], P('dp'), may hold values from 0 to 361
- value_target: int32 [32, 2], P('dp'), may hold values from 0 to 600
- reward_target: int32 [32, 2], P('dp'), may hold values from 0 to 600
- kernel_first: float32 [3, 3, 256, 256], P(None, None, 'dp', 'mp'), may hold values from -6 to 6
- kernel_second: float32 [3, 3, 256, 256], P(None, None, 'dp', 'mp'), may hold values from -6 to 6
- head_weight: float32 [2, 256, 601], P('mp', 'dp'), may hold values from -6 to 6
- action_embed: float32 [2, 256], P('mp', 'dp'), may hold values from -6 to 6
- first_mean: float32 [3, 3, 256, 256], P(None, None, 'dp', 'mp'), may hold values from -0.00061035156 to 0.00061035156
- first_square: float32 [3, 3, 256, 256], P(None, None, 'dp', 'mp'), may hold values from 1e-09 to 1e-06
- second_mean: float32 [3, 3, 256, 256], P(None, None, 'dp', 'mp'), may hold values from -0.00061035156 to 0.00061035156
- second_square: float32 [3, 3, 256, 256], P(None, None, 'dp', 'mp'), may hold values from 1e-09 to 1e-06
- head_mean: float32 [2, 256, 601], P('mp', 'dp'), may hold values from -0.0029296875 to 0.0029296875
- head_square: float32 [2, 256, 601], P('mp', 'dp'), may hold values from 1e-08 to 1e-06
- embed_mean: float32 [2, 256], P('mp', 'dp'), may hold values from -0.0017089844 to 0.0017089844
- embed_square: float32 [2, 256], P('mp', 'dp'), may hold values from 1e-09 to 1e-06
Outputs:
- kernel_first_new: float32 [3, 3, 256, 256], P(None, None, 'dp', 'mp')
- kernel_second_new: float32 [3, 3, 256, 256], P(None, None, 'dp', 'mp')
- head_weight_new: float32 [2, 256, 601], P('mp', 'dp')
- action_embed_new: float32 [2, 256], P('mp', 'dp')
- first_mean_new: float32 [3, 3, 256, 256], P(None, None, 'dp', 'mp')
- first_square_new: float32 [3, 3, 256, 256], P(None, None, 'dp', 'mp')
- second_mean_new: float32 [3, 3, 256, 256], P(None, None, 'dp', 'mp')
- second_square_new: float32 [3, 3, 256, 256], P(None, None, 'dp', 'mp')
- head_mean_new: float32 [2, 256, 601], P('mp', 'dp')
- head_square_new: float32 [2, 256, 601], P('mp', 'dp')
- embed_mean_new: float32 [2, 256], P('mp', 'dp')
- embed_square_new: float32 [2, 256], P('mp', 'dp')
- first_grad: float32 [3, 3, 256, 256], P(None, None, 'dp', 'mp')
- second_grad: float32 [3, 3, 256, 256], P(None, None, 'dp', 'mp')
- head_grad: float32 [2, 256, 601], P('mp', 'dp')
- embed_grad: float32 [2, 256], P('mp', 'dp')
Inputs may be any that keep to these rules, and one draw needn't show every extreme that they name: `actions`: the value 361 stands for a pass.
All inputs are finite; a program needn't handle non-finite values.
Results may differ from a plain program's by a relative error of at most 0.02.
Values may be sent and summed in bfloat16 or wider, within the bound.
No kernel may reach another device: no remote copies, remote signals or barrier semaphores. Data moves between devices by JAX's collectives and lax.ppermute only.
A program may use at most 64 MiB of HBM per device.

v0:
```python
import jax
import jax.numpy as jnp
from jax import lax
from jax.sharding import PartitionSpec as P

CHANNELS = 256
head_scale = 4.0
soft_cap = 15.0
eps_norm = 1e-05
beta_one = 0.9
beta_two = 0.999
step_size = 0.1
eps_adam = 1e-08


def conv_apply(field, kernel, layout):
    return lax.conv_general_dilated(
        field,
        kernel,
        (1, 1),
        "SAME",
        dimension_numbers=("NHWC", layout, "NHWC"),
        preferred_element_type=jnp.float32,
    )


def gate_slope(pre):
    sig = jax.nn.sigmoid(pre)
    return sig * (1.0 + pre * (1.0 - sig))


def tap_products(field, grad, field_rows):
    side = field.shape[1]
    padded = jnp.pad(field, ((0, 0), (1, 1), (1, 1), (0, 0)))
    flat_grad = grad.reshape(-1, grad.shape[3])
    blocks = []
    for offset in range(9):
        row_start = offset // 3
        col_start = offset % 3
        window = padded[:, row_start : row_start + side, col_start : col_start + side, :].reshape(
            -1, field.shape[3]
        )
        if field_rows:
            blocks.append(
                lax.dot_general(
                    window, flat_grad, (((0,), (0,)), ((), ())), preferred_element_type=jnp.float32
                )
            )
        else:
            blocks.append(
                lax.dot_general(
                    flat_grad, window, (((0,), (0,)), ((), ())), preferred_element_type=jnp.float32
                )
            )
    stacked = jnp.stack(blocks)
    return stacked.reshape(3, 3, stacked.shape[1], stacked.shape[2])


def action_planes(move, board):
    cells = board * board
    plane = (lax.broadcasted_iota(jnp.int32, (move.shape[0], cells), 1) == move[:, None]).astype(
        jnp.float32
    )
    passed = (move == cells).astype(jnp.float32)
    return (plane.reshape(move.shape[0], board, board, 1), passed[:, None, None, None])


def head_backward(state, head_used, value_now, reward_now, total):
    pooled = jnp.mean(state, axis=(1, 2)).astype(jnp.bfloat16)
    raw = head_scale * jnp.stack(
        [
            jnp.dot(pooled, head_used[0], preferred_element_type=jnp.float32),
            jnp.dot(pooled, head_used[1], preferred_element_type=jnp.float32),
        ]
    )
    squashed = jnp.tanh(raw / soft_cap)
    raised = jnp.exp(soft_cap * squashed)
    chances = raised / jnp.sum(raised, axis=2, keepdims=True)
    targets = jnp.stack([value_now, reward_now])
    picked = (lax.broadcasted_iota(jnp.int32, raw.shape, 2) == targets[:, :, None]).astype(
        jnp.float32
    )
    logit_grad = ((chances - picked) * (1.0 - squashed * squashed) / total).astype(jnp.bfloat16)
    pooled_grad = head_scale * (
        jnp.dot(logit_grad[0], head_used[0].T, preferred_element_type=jnp.float32)
        + jnp.dot(logit_grad[1], head_used[1].T, preferred_element_type=jnp.float32)
    )
    return (pooled, logit_grad, pooled_grad)


def adam_update(param, grad, mean, square):
    mean_new = beta_one * mean + (1.0 - beta_one) * grad
    square_new = beta_two * square + (1.0 - beta_two) * grad * grad
    param_new = param - step_size * mean_new / (jnp.sqrt(square_new) + eps_adam)
    return (param_new, mean_new, square_new)


def local(
    hidden_state,
    actions,
    value_target,
    reward_target,
    kernel_first,
    kernel_second,
    head_weight,
    action_embed,
    first_mean,
    first_square,
    second_mean,
    second_square,
    head_mean,
    head_square,
    embed_mean,
    embed_square,
):
    total = hidden_state.shape[0] * lax.axis_size("dp")
    board = hidden_state.shape[1]
    cells = board * board
    scale = (9.0 * CHANNELS) ** (-0.5)
    first_used, second_used, head_used, embed_used = (
        lax.all_gather(kernel_first.astype(jnp.bfloat16), "dp", axis=2, tiled=True),
        lax.all_gather(kernel_second.astype(jnp.bfloat16), "dp", axis=2, tiled=True),
        lax.all_gather(head_weight.astype(jnp.bfloat16), "dp", axis=1, tiled=True),
        lax.all_gather(action_embed.astype(jnp.bfloat16), "dp", axis=1, tiled=True),
    )
    first_used, second_used, head_used, embed_used = (
        lax.all_gather(first_used, "mp", axis=3, tiled=True),
        lax.all_gather(second_used, "mp", axis=3, tiled=True),
        lax.all_gather(head_used, "mp", axis=0, tiled=True),
        lax.all_gather(embed_used, "mp", axis=0, tiled=True),
    )
    count = hidden_state.shape[0] // lax.axis_size("mp")
    begin = lax.axis_index("mp") * count
    states = lax.dynamic_slice_in_dim(hidden_state, begin, count, 0)
    moves = lax.dynamic_slice_in_dim(actions, begin, count, 0)
    values = lax.dynamic_slice_in_dim(value_target, begin, count, 0)
    rewards = lax.dynamic_slice_in_dim(reward_target, begin, count, 0)
    unroll = moves.shape[1]
    embed = embed_used.astype(jnp.float32)
    state = states.astype(jnp.float32)
    saved = []
    for position in range(unroll):
        plane, passed = action_planes(moves[:, position], board)
        mixed = state + plane * embed[0] + passed * embed[1]
        conv_input = mixed.astype(jnp.bfloat16)
        pre = scale * conv_apply(conv_input, first_used, "HWIO")
        hidden = jax.nn.silu(pre).astype(jnp.bfloat16)
        branch = conv_apply(hidden, second_used, "HWOI")
        summed = mixed + scale * branch
        factor = lax.rsqrt(jnp.mean(summed * summed, axis=(1, 2, 3), keepdims=True) + eps_norm)
        state = summed * factor
        pooled, logit_grad, pooled_grad = head_backward(
            state, head_used, values[:, position], rewards[:, position], total
        )
        saved.append(
            (
                plane,
                passed,
                conv_input,
                pre,
                hidden,
                summed,
                factor,
                pooled,
                logit_grad,
                pooled_grad,
            )
        )
    first_grad = jnp.zeros(first_used.shape, jnp.float32)
    second_grad = jnp.zeros(second_used.shape, jnp.float32)
    head_grad = jnp.zeros(head_used.shape, jnp.float32)
    embed_grad = jnp.zeros(embed_used.shape, jnp.float32)
    carry = jnp.zeros(states.shape, jnp.float32)
    for position in range(unroll - 1, -1, -1):
        plane, passed, conv_input, pre, hidden, summed, factor, pooled, logit_grad, pooled_grad = (
            saved[position]
        )
        state_grad = carry + pooled_grad[:, None, None, :] / cells
        summed_grad = factor * state_grad - factor * factor * factor * summed * jnp.mean(
            state_grad * summed, axis=(1, 2, 3), keepdims=True
        )
        branch_grad = summed_grad.astype(jnp.bfloat16)
        hidden_grad = scale * conv_apply(branch_grad, second_used[::-1, ::-1], "HWIO")
        inner_grad = (hidden_grad * gate_slope(pre)).astype(jnp.bfloat16)
        input_grad = conv_apply(inner_grad, first_used[::-1, ::-1], "HWOI")
        carry = summed_grad + scale * input_grad
        first_grad = first_grad + scale * tap_products(conv_input, inner_grad, True)
        second_grad = second_grad + scale * tap_products(hidden, branch_grad, False)
        head_grad = head_grad + head_scale * jnp.stack(
            [
                lax.dot_general(
                    pooled,
                    logit_grad[0],
                    (((0,), (0,)), ((), ())),
                    preferred_element_type=jnp.float32,
                ),
                lax.dot_general(
                    pooled,
                    logit_grad[1],
                    (((0,), (0,)), ((), ())),
                    preferred_element_type=jnp.float32,
                ),
            ]
        )
        embed_grad = embed_grad + jnp.stack(
            [jnp.sum(plane * carry, axis=(0, 1, 2)), jnp.sum(passed * carry, axis=(0, 1, 2))]
        )
    first_grad, second_grad, head_grad, embed_grad = (
        lax.psum_scatter(first_grad, "mp", scatter_dimension=3, tiled=True),
        lax.psum_scatter(second_grad, "mp", scatter_dimension=3, tiled=True),
        lax.psum_scatter(head_grad, "mp", scatter_dimension=0, tiled=True),
        lax.psum_scatter(embed_grad, "mp", scatter_dimension=0, tiled=True),
    )
    first_grad, second_grad, head_grad, embed_grad = (
        lax.psum_scatter(first_grad, "dp", scatter_dimension=2, tiled=True),
        lax.psum_scatter(second_grad, "dp", scatter_dimension=2, tiled=True),
        lax.psum_scatter(head_grad, "dp", scatter_dimension=1, tiled=True),
        lax.psum_scatter(embed_grad, "dp", scatter_dimension=1, tiled=True),
    )
    first_new, first_mean_new, first_square_new = adam_update(
        kernel_first, first_grad, first_mean, first_square
    )
    second_new, second_mean_new, second_square_new = adam_update(
        kernel_second, second_grad, second_mean, second_square
    )
    head_new, head_mean_new, head_square_new = adam_update(
        head_weight, head_grad, head_mean, head_square
    )
    embed_new, embed_mean_new, embed_square_new = adam_update(
        action_embed, embed_grad, embed_mean, embed_square
    )
    return (
        first_new,
        second_new,
        head_new,
        embed_new,
        first_mean_new,
        first_square_new,
        second_mean_new,
        second_square_new,
        head_mean_new,
        head_square_new,
        embed_mean_new,
        embed_square_new,
        first_grad,
        second_grad,
        head_grad,
        embed_grad,
    )


def solution(mesh):
    placed = (
        P("dp", None, None, None),
        P("dp", None),
        P("dp", None),
        P("dp", None),
        P(None, None, "dp", "mp"),
        P(None, None, "dp", "mp"),
        P("mp", "dp", None),
        P("mp", "dp"),
        P(None, None, "dp", "mp"),
        P(None, None, "dp", "mp"),
        P(None, None, "dp", "mp"),
        P(None, None, "dp", "mp"),
        P("mp", "dp", None),
        P("mp", "dp", None),
        P("mp", "dp"),
        P("mp", "dp"),
    )
    return jax.shard_map(
        local,
        mesh=mesh,
        in_specs=placed,
        out_specs=(
            P(None, None, "dp", "mp"),
            P(None, None, "dp", "mp"),
            P("mp", "dp", None),
            P("mp", "dp"),
            P(None, None, "dp", "mp"),
            P(None, None, "dp", "mp"),
            P(None, None, "dp", "mp"),
            P(None, None, "dp", "mp"),
            P("mp", "dp", None),
            P("mp", "dp", None),
            P("mp", "dp"),
            P("mp", "dp"),
            P(None, None, "dp", "mp"),
            P(None, None, "dp", "mp"),
            P("mp", "dp", None),
            P("mp", "dp"),
        ),
        check_vma=False,
    )
```

profile of v0, /device:TPU:0, one launch (start us, length us, event | category | flops | bytes accessed | tf_op | source)
XLA Modules:
  0.0 581.1 jit_solution(16968905555778703401)
XLA Ops:
  7.3 1.0 convert_element_type.150
  8.3 48.3 %all_gather.26 = bf16[3,3,256,128]{3,2,1,0:T(8,128)(2,1)} all-gather(bf16[3,3,16,128]{3,2,1,0:T(8,128)(2,1)S(1)} %convert_element_type.150), channel_id=1, replica_groups=mesh['dp'=16,'mp'=2] {'dp'}, dimensions={2}, use_global_device_ids=true | all-gather | bytes 626688 | tf_op jit(solution)/shard_map/all_gather | solution.py:121
  56.6 0.9 convert_element_type.152
  57.5 41.0 %all_gather.28 = bf16[3,3,256,128]{3,2,1,0:T(8,128)(2,1)} all-gather(bf16[3,3,16,128]{3,2,1,0:T(8,128)(2,1)S(1)} %convert_element_type.152), channel_id=1, replica_groups=mesh['dp'=16,'mp'=2] {'dp'}, dimensions={2}, use_global_device_ids=true | all-gather | bytes 626688 | tf_op jit(solution)/shard_map/all_gather | solution.py:122
  98.6 0.6 dynamic-slice
  100.1 38.8 %all-reduce.4 = bf16[256]{0:T(256)(128)(2,1)S(1)} all-reduce(bf16[256]{0:T(256)(128)(2,1)S(1)} %dynamic-update-slice), channel_id=1, replica_groups=mesh['dp'=16,'mp'=2] {'dp'}, use_global_device_ids=true, to_apply=%add.4 | all-reduce | flops 256 | bytes 1024
  138.9 1.8 all-gather
  140.8 0.6 fusion.358
  142.6 0.7 fusion.265
  143.7 0.7 fusion.266
  144.4 37.2 %all_gather.30 = bf16[1,256,601]{2,1,0:T(8,128)(2,1)S(1)} all-gather(bf16[1,16,601]{2,1,0:T(8,128)(2,1)S(1)} %convert_element_type.157), channel_id=1, replica_groups=mesh['dp'=16,'mp'=2] {'dp'}, dimensions={1}, use_global_device_ids=true | all-gather | bytes 326944 | tf_op jit(solution)/shard_map/all_gather | solution.py:123
  181.6 0.6 fusion.356
  183.4 1.4 add_reduce_fusion
  184.8 1.4 add_reduce_fusion.1
  186.2 2.4 all_gather.31
  188.6 0.8 fusion.61
  189.5 2.0 fusion.6
  192.3 2.0 convolution_multiply_fusion.3
  194.8 0.8 multiply_reduce_fusion.8
  196.4 0.7 copy-done.1
  197.4 2.1 fusion.5
  199.5 0.8 select_bitcast_fusion.2
  200.4 0.8 convolution_multiply_fusion.2
  201.7 0.8 multiply_reduce_fusion.7
  205.3 0.7 multiply_reduce_fusion.5
  206.8 0.7 fusion.126
  207.8 2.1 fusion.7
  210.6 0.8 convolution_multiply_fusion.1
  211.9 0.8 multiply_reduce_fusion.3
  213.3 0.8 fusion.348
  214.2 1.0 pad.29
  215.3 0.7 slice.243
  216.4 1.2 fusion
  218.3 1.2 fusion.17
  219.6 1.2 fusion.16
  220.8 1.3 fusion.15
  222.1 1.2 fusion.14
  223.4 1.2 fusion.13
  224.6 1.2 fusion.12
  225.9 1.2 fusion.11
  227.1 1.3 fusion.10
  228.4 1.2 fusion.9
  229.8 0.9 reshape.830
  230.6 1.0 slice_bitcast_fusion.9
  231.6 1.2 fusion.26
  235.6 2.0 add_multiply_fusion
  237.7 0.8 copy-done.8
  238.7 2.0 fusion.8
  247.1 1.7 add_multiply_fusion.1
  250.2 0.8 convolution_multiply_fusion
  251.8 2.5 all-reduce.5
  254.2 0.7 constant_dynamic-slice_fusion.4
  254.9 0.8 copy.106
  255.8 0.7 reduce-scatter.20.cloned.1.call-update
  256.5 0.7 reduce-scatter.16.cloned.1.call-update
  257.3 1.5 reduce-scatter.10.cloned.1.call-done
  258.8 80.4 %reduce-scatter.22.cloned.1.call-done = f32[16,1]{1,0:T(8,128)} async-done(((f32[256,1]{1,0:T(8,128)}), f32[16,1]{1,0:T(8,128)}) %reduce-scatter.22.cloned.1.call-update) | async-done | bytes 80
  339.2 0.8 copy.107
  340.5 75.6 %reduce-scatter.20.cloned.1.call-done = f32[1,16,601]{2,1,0:T(8,128)} async-done(((f32[1,256,601]{2,1,0:T(8,128)}), f32[1,16,601]{2,1,0:T(8,128)}) %reduce-scatter.20.cloned.1.call-update) | async-done | bytes 38480 | tf_op jit(solution)/shard_map/reduce_scatter | solution.py:217
  416.1 1.4 divide_subtract_fusion.2
  417.6 77.1 %reduce-scatter.16.cloned.1.call-done = f32[3,3,16,128]{3,2,1,0:T(8,128)} async-done(((f32[3,3,256,128]{3,2,1,0:T(8,128)}), f32[3,3,16,128]{3,2,1,0:T(8,128)}) %reduce-scatter.16.cloned.1.call-update) | async-done | bytes 73744 | tf_op jit(solution)/shard_map/reduce_scatter | solution.py:216
  494.6 1.6 divide_subtract_fusion
  496.2 76.8 %reduce-scatter.12.cloned.1.call-done = f32[3,3,16,128]{3,2,1,0:T(8,128)} async-done(((f32[3,3,256,128]{3,2,1,0:T(8,128)}), f32[3,3,16,128]{3,2,1,0:T(8,128)}) %reduce-scatter.12.cloned.1.call-update) | async-done | bytes 73744 | tf_op jit(solution)/shard_map/reduce_scatter | solution.py:215
  573.0 1.6 divide_subtract_fusion.1
  (206 shorter events, 20.9 us)
Async XLA Ops:
  7.2 136.1 %copy-start = (bf16[2,19,19,256]{3,0,2,1:T(2,128)(2,1)S(1)}, bf16[2,19,19,256]{3,0,2,1:T(2,128)(2,1)}, u32[]{:S(2)}) copy-start(bf16[2,19,19,256]{3,0,2,1:T(2,128)(2,1)} %param.16) | copy-start | bytes 1108996
  7.2 91.4 %copy-start.38 = (u32[32]{0:T(128)S(1)}, u32[32]{0:T(128)}, u32[]{:S(2)}) copy-start(u32[32]{0:T(128)} %constant.145) | copy-start | bytes 388
  7.2 91.4 %copy-start.28 = (f32[1,16]{1,0:T(1,128)S(1)}, f32[1,16]{1,0:T(1,128)}, u32[]{:S(2)}) copy-start(f32[1,16]{1,0:T(1,128)} %param.23) | copy-start | bytes 196
  7.2 133.5 %copy-start.36 = (s32[2,2]{1,0:T(2,128)S(1)}, s32[2,2]{1,0:T(2,128)}, u32[]{:S(2)}) copy-start(s32[2,2]{1,0:T(2,128)} %param.17) | copy-start | bytes 52
  7.2 137.1 %copy-start.17 = (f32[1,16,601]{2,1,0:T(8,128)S(1)}, f32[1,16,601]{2,1,0:T(8,128)}, u32[]{:S(2)}) copy-start(f32[1,16,601]{2,1,0:T(8,128)} %param.22) | copy-start | bytes 115396
  7.2 174.4 %copy-start.32 = (s32[2,2]{1,0:T(2,128)S(1)}, s32[2,2]{1,0:T(2,128)}, u32[]{:S(2)}) copy-start(s32[2,2]{1,0:T(2,128)} %param.18) | copy-start | bytes 52
  7.3 174.4 %copy-start.31 = (s32[2,2]{1,0:T(2,128)S(1)}, s32[2,2]{1,0:T(2,128)}, u32[]{:S(2)}) copy-start(s32[2,2]{1,0:T(2,128)} %param.19) | copy-start | bytes 52
  7.3 182.2 %all-gather.4.cloned.1.call-start = ((), (), s32[]{:S(2)}) async-start(), calls=%async_computation.7 | async-start | bytes 1769472 | tf_op jit(solution)/shard_map/all_gather | solution.py:127
  56.6 135.1 %all-gather.6.cloned.1.call-start = ((), (), s32[]{:S(2)}) async-start(), calls=%async_computation.8 | async-start | bytes 1769472 | tf_op jit(solution)/shard_map/all_gather | solution.py:128
  98.5 157.2 %reduce-scatter.18.cloned.1.call-start = ((), (), s32[]{:S(2)}) async-start(), calls=%async_computation.13 | async-start | bytes 1966080 | tf_op jit(solution)/shard_map/reduce_scatter | solution.py:211
  181.6 7.9 %copy-start.26 = (pred[8,3]{0,1:T(4,128)(4,1)S(1)}, pred[8,3]{0,1:T(4,128)(4,1)}, u32[]{:S(2)}) copy-start(pred[8,3]{0,1:T(4,128)(4,1)} %constant.135) | copy-start | bytes 76
  191.5 0.8 copy-start.9
  196.4 0.7 copy-start.1
  197.4 3.0 copy-start.35
  199.5 0.9 copy-start.11
  204.5 3.3 copy-start.12
  207.8 2.8 copy-start.33
  209.9 0.7 copy-start.5
  215.3 2.3 copy-start.7
  217.7 38.8 %reduce-scatter.14.cloned.1.call-start = ((), (), s32[]{:S(2)}) async-start(), calls=%async_computation.11 | async-start | bytes 3538944 | tf_op jit(solution)/shard_map/reduce_scatter | solution.py:210
  227.1 2.5 copy-start.3
  230.6 2.2 copy-start.16
  233.2 0.9 copy-start.4
  237.6 0.9 copy-start.8
  237.6 1.1 copy-start.10
  237.6 1.2 copy-start.19
  237.6 3.1 copy-start.6
  237.6 3.8 copy-start.15
  237.6 21.2 %reduce-scatter.10.cloned.1.call-start = ((), (), s32[]{:S(2)}) async-start(), calls=%async_computation.9 | async-start | bytes 3538944 | tf_op jit(solution)/shard_map/reduce_scatter | solution.py:209
  243.5 1.0 copy-start.2
  248.8 0.7 copy-start.37
  248.8 1.4 copy-start.34
  248.9 90.3 %reduce-scatter.22.cloned.1.call-start = ((), (), s32[]{:S(2)}) async-start(), calls=%async_computation.15 | async-start | bytes 139264
  251.5 88.5 %copy-start.29 = (f32[1,16]{1,0:T(1,128)S(1)}, f32[1,16]{1,0:T(1,128)}, u32[]{:S(2)}) copy-start(f32[1,16]{1,0:T(1,128)} %param.30) | copy-start | bytes 196
  251.5 88.5 %copy-start.30 = (f32[1,16]{1,0:T(1,128)S(1)}, f32[1,16]{1,0:T(1,128)}, u32[]{:S(2)}) copy-start(f32[1,16]{1,0:T(1,128)} %param.31) | copy-start | bytes 196
  251.5 164.7 %copy-start.18 = (f32[1,16,601]{2,1,0:T(8,128)S(1)}, f32[1,16,601]{2,1,0:T(8,128)}, u32[]{:S(2)}) copy-start(f32[1,16,601]{2,1,0:T(8,128)} %param.22) | copy-start | bytes 115396
  251.5 164.6 %copy-start.24 = (f32[1,16,601]{2,1,0:T(8,128)S(1)}, f32[1,16,601]{2,1,0:T(8,128)}, u32[]{:S(2)}) copy-start(f32[1,16,601]{2,1,0:T(8,128)} %param.28) | copy-start | bytes 115396
  251.5 164.6 %copy-start.25 = (f32[1,16,601]{2,1,0:T(8,128)S(1)}, f32[1,16,601]{2,1,0:T(8,128)}, u32[]{:S(2)}) copy-start(f32[1,16,601]{2,1,0:T(8,128)} %param.29) | copy-start | bytes 115396
  251.5 243.1 %copy-start.13 = (f32[3,3,16,128]{3,2,1,0:T(8,128)S(1)}, f32[3,3,16,128]{3,2,1,0:T(8,128)}, u32[]{:S(2)}) copy-start(f32[3,3,16,128]{3,2,1,0:T(8,128)} %param.21) | copy-start | bytes 221188
  251.5 243.1 %copy-start.20 = (f32[3,3,16,128]{3,2,1,0:T(8,128)S(1)}, f32[3,3,16,128]{3,2,1,0:T(8,128)}, u32[]{:S(2)}) copy-start(f32[3,3,16,128]{3,2,1,0:T(8,128)} %param.26) | copy-start | bytes 221188
  251.5 243.1 %copy-start.21 = (f32[3,3,16,128]{3,2,1,0:T(8,128)S(1)}, f32[3,3,16,128]{3,2,1,0:T(8,128)}, u32[]{:S(2)}) copy-start(f32[3,3,16,128]{3,2,1,0:T(8,128)} %param.27) | copy-start | bytes 221188
  251.5 321.5 %copy-start.14 = (f32[3,3,16,128]{3,2,1,0:T(8,128)S(1)}, f32[3,3,16,128]{3,2,1,0:T(8,128)}, u32[]{:S(2)}) copy-start(f32[3,3,16,128]{3,2,1,0:T(8,128)} %param.20) | copy-start | bytes 221188
  251.6 321.5 %copy-start.22 = (f32[3,3,16,128]{3,2,1,0:T(8,128)S(1)}, f32[3,3,16,128]{3,2,1,0:T(8,128)}, u32[]{:S(2)}) copy-start(f32[3,3,16,128]{3,2,1,0:T(8,128)} %param.24) | copy-start | bytes 221188
  251.6 321.4 %copy-start.23 = (f32[3,3,16,128]{3,2,1,0:T(8,128)S(1)}, f32[3,3,16,128]{3,2,1,0:T(8,128)}, u32[]{:S(2)}) copy-start(f32[3,3,16,128]{3,2,1,0:T(8,128)} %param.25) | copy-start | bytes 221188
  255.7 160.4 %reduce-scatter.20.cloned.1.call-start = ((), (), s32[]{:S(2)}) async-start(), calls=%async_computation.14 | async-start | bytes 696320 | tf_op jit(solution)/shard_map/reduce_scatter | solution.py:217
  256.5 238.2 %reduce-scatter.16.cloned.1.call-start = ((), (), s32[]{:S(2)}) async-start(), calls=%async_computation.12 | async-start | bytes 1253376 | tf_op jit(solution)/shard_map/reduce_scatter | solution.py:216
  257.2 315.8 %reduce-scatter.12.cloned.1.call-start = ((), (), s32[]{:S(2)}) async-start(), calls=%async_computation.10 | async-start | bytes 1253376 | tf_op jit(solution)/shard_map/reduce_scatter | solution.py:215
  340.0 234.7 %copy-start.27 = (f32[1,16]{1,0:T(1,128)}, f32[1,16]{1,0:T(1,128)S(1)}, u32[]{:S(2)}) copy-start(f32[1,16]{1,0:T(1,128)S(1)} %copy.107) | copy-start | bytes 196
Sparse Core Ops, SparseCore 0:
  56.7 4.7 all-gather.3
  98.7 6.9 all-gather.5
  217.8 6.4 reduce-scatter.17
  237.7 7.6 reduce-scatter.13
  249.0 9.7 reduce-scatter.9
  260.9 78.2 reduce-scatter.21
  342.0 74.0 reduce-scatter.19
  419.0 75.6 reduce-scatter.15
  497.5 75.4 reduce-scatter.11
where the time goes:
time: 582 us; the launch traced here: 581 us
  waiting for transfers between devices  313 us (54%)
  blocking collectives  172 us (30%)
  matrix products  33.7 us (6%)
  other arithmetic  24.3 us (4%)
  between operations  19.6 us (3%)
  local copies, waits for them, and re-layouts  18.2 us (3%)
    unnamed x10, waiting for transfers between devices  81.8 us
    reduce_scatter x1, waiting for transfers between devices, local(): lax.psum_scatter(second_grad, 'dp', scatter_dimension=2, tiled=True)  77.1 us
    reduce_scatter x1, waiting for transfers between devices, local(): lax.psum_scatter(first_grad, 'dp', scatter_dimension=2, tiled=True)  76.8 us
    reduce_scatter x1, waiting for transfers between devices, local(): lax.psum_scatter(head_grad, 'dp', scatter_dimension=1, tiled=True)  75.6 us
    all_gather x1, blocking collectives, local(): lax.all_gather(kernel_first.astype(jnp.bfloat16), 'dp', axis=2, tiled=True)  48.3 us
    unnamed x2, blocking collectives  41.3 us
    all_gather x1, blocking collectives, local(): lax.all_gather(kernel_second.astype(jnp.bfloat16), 'dp', axis=2, tiled=True)  41 us
    all_gather x1, blocking collectives, local(): lax.all_gather(head_weight.astype(jnp.bfloat16), 'dp', axis=1, tiled=True)  37.2 us
  transfers between devices with their start and end apart: 9, of which 5 were waited for; matrix products, arithmetic and copies ran while one was open for 8% of the time, Pallas kernels for 0%

commit v1 on v0

--- a/solution.py
+++ b/solution.py
@@ -11,6 +11,11 @@
 beta_two = 0.999
 step_size = 0.1
 eps_adam = 1e-08
+
+
+def swapped_in(x, axis, d):
+    sent = jnp.stack([x] * lax.axis_size(axis))
+    return jnp.concatenate(lax.all_to_all(sent, axis, 0, 0), axis=d)
 
 
 def conv_apply(field, kernel, layout):
@@ -119,7 +124,7 @@
     scale = (9.0 * CHANNELS) ** (-0.5)
     first_used, second_used, head_used, embed_used = (
         lax.all_gather(kernel_first.astype(jnp.bfloat16), "dp", axis=2, tiled=True),
-        lax.all_gather(kernel_second.astype(jnp.bfloat16), "dp", axis=2, tiled=True),
+        swapped_in(kernel_second.astype(jnp.bfloat16), "dp", 2),
         lax.all_gather(head_weight.astype(jnp.bfloat16), "dp", axis=1, tiled=True),
         lax.all_gather(action_embed.astype(jnp.bfloat16), "dp", axis=1, tiled=True),
     )

time: 582 us -> 556 us (0.955)
  blocking collectives: 172 us -> 134 us
    all_gather x1 -> x0, blocking collectives: 41 us -> none  [local(): lax.all_gather(kernel_second.astype(jnp.bfloat16), 'dp', axis=2, tiled=True)]
  transfers between devices with their start and end apart: 9 -> 10, of which waited for: 5 -> 6; matrix products, arithmetic and copies ran while one was open for 8% -> 9% of each run, Pallas kernels for 0% -> 0%
where the time goes in v1:
time: 556 us; the launch traced here: 555 us
  waiting for transfers between devices  318 us (57%)
  blocking collectives  134 us (24%)
  matrix products  33.9 us (6%)
  other arithmetic  24.2 us (4%)
  local copies, waits for them, and re-layouts  20.8 us (4%)
  between operations  19.7 us (4%)
    unnamed x10, waiting for transfers between devices  81.6 us
    reduce_scatter x1, waiting for transfers between devices, local(): lax.psum_scatter(second_grad, 'dp', scatter_dimension=2, tiled=True)  76.9 us
    reduce_scatter x1, waiting for transfers between devices, local(): lax.psum_scatter(first_grad, 'dp', scatter_dimension=2, tiled=True)  76.7 us
    reduce_scatter x1, waiting for transfers between devices, local(): lax.psum_scatter(head_grad, 'dp', scatter_dimension=1, tiled=True)  75.5 us
    all_gather x1, blocking collectives, local(): lax.all_gather(kernel_first.astype(jnp.bfloat16), 'dp', axis=2, tiled=True)  48.3 us
    unnamed x2, blocking collectives  44.5 us
    all_gather x1, blocking collectives, local(): lax.all_gather(head_weight.astype(jnp.bfloat16), 'dp', axis=1, tiled=True)  37.2 us
    dot_general x18, matrix products, tap_products(): lax.dot_general(flat_grad, window, (((0,), (0,)), ((), ())), preferred_el...  14.9 us
  transfers between devices with their start and end apart: 10, of which 6 were waited for; matrix products, arithmetic and copies ran while one was open for 9% of the time, Pallas kernels for 0%

profile of v1, /device:TPU:0, one launch (start us, length us, event | category | flops | bytes accessed | tf_op | source)
XLA Modules:
  0.0 555.1 jit_solution(12873333255535824534)
XLA Ops:
  7.3 0.9 convert_element_type.150
  8.2 48.3 %all_gather.23 = bf16[3,3,256,128]{3,2,1,0:T(8,128)(2,1)} all-gather(bf16[3,3,16,128]{3,2,1,0:T(8,128)(2,1)S(1)} %convert_element_type.150), channel_id=1, replica_groups=mesh['dp'=16,'mp'=2] {'dp'}, dimensions={2}, use_global_device_ids=true | all-gather | bytes 626688 | tf_op jit(solution)/shard_map/all_gather | solution.py:126
  56.5 0.9 convert_element_type.152
  57.4 0.9 stack.203
  58.3 3.7 all-to-all-start
  65.6 42.1 %all-reduce.4 = bf16[256]{0:T(256)(128)(2,1)S(1)} all-reduce(bf16[256]{0:T(256)(128)(2,1)S(1)} %dynamic-update-slice), channel_id=1, replica_groups=mesh['dp'=16,'mp'=2] {'dp'}, use_global_device_ids=true, to_apply=%add.4 | all-reduce | flops 256 | bytes 1024
  107.6 1.8 all-gather
  109.4 0.7 fusion.265
  111.0 37.2 %all_gather.26 = bf16[1,256,601]{2,1,0:T(8,128)(2,1)S(1)} all-gather(bf16[1,16,601]{2,1,0:T(8,128)(2,1)S(1)} %convert_element_type.157), channel_id=1, replica_groups=mesh['dp'=16,'mp'=2] {'dp'}, dimensions={1}, use_global_device_ids=true | all-gather | bytes 326944 | tf_op jit(solution)/shard_map/all_gather | solution.py:128
  149.6 1.4 add_reduce_fusion
  151.0 1.4 add_reduce_fusion.1
  152.4 0.7 fusion.266
  153.0 2.3 all_gather.27
  155.3 0.9 copy.93
  156.5 0.8 fusion.61
  157.3 2.0 fusion.6
  160.5 0.7 slice_bitcast_fusion.8
  161.2 2.0 all-gather.6.cloned.1.call-done
  163.3 2.0 convolution_multiply_fusion.3
  165.8 0.8 multiply_reduce_fusion.8
  167.4 0.7 copy-done.1
  168.4 2.1 fusion.5
  170.5 0.8 select_bitcast_fusion.2
  171.4 0.8 convolution_multiply_fusion.2
  172.7 0.8 multiply_reduce_fusion.7
  176.3 0.7 multiply_reduce_fusion.5
  177.8 0.8 fusion.126
  178.8 2.1 fusion.7
  181.6 0.7 convolution_multiply_fusion.1
  182.9 0.8 multiply_reduce_fusion.3
  184.3 0.8 fusion.348
  185.2 1.0 pad.29
  186.3 0.7 slice.243
  187.4 1.2 fusion
  188.9 1.4 fusion.17
  190.3 1.3 fusion.16
  191.7 1.2 fusion.15
  192.9 1.2 fusion.14
  194.1 1.2 fusion.13
  195.4 1.3 fusion.12
  196.6 1.2 fusion.11
  197.9 1.3 fusion.10
  199.2 1.2 fusion.9
  200.6 0.9 reshape.840
  201.5 1.0 slice_bitcast_fusion.9
  202.5 1.2 fusion.26
  206.4 2.0 add_multiply_fusion
  208.6 0.8 copy-done.8
  209.6 2.0 fusion.8
  218.0 1.7 add_multiply_fusion.1
  221.1 0.8 convolution_multiply_fusion
  222.6 2.5 all-reduce.5
  225.7 0.8 copy.109
  226.6 0.7 reduce-scatter.20.cloned.1.call-update
  227.4 0.7 reduce-scatter.16.cloned.1.call-update
  228.1 5.1 reduce-scatter.10.cloned.1.call-done
  233.2 80.2 %reduce-scatter.22.cloned.1.call-done = f32[16,1]{1,0:T(8,128)} async-done(((f32[256,1]{1,0:T(8,128)}), f32[16,1]{1,0:T(8,128)}) %reduce-scatter.22.cloned.1.call-update) | async-done | bytes 80
  313.4 0.8 copy.110
  314.7 75.5 %reduce-scatter.20.cloned.1.call-done = f32[1,16,601]{2,1,0:T(8,128)} async-done(((f32[1,256,601]{2,1,0:T(8,128)}), f32[1,16,601]{2,1,0:T(8,128)}) %reduce-scatter.20.cloned.1.call-update) | async-done | bytes 38480 | tf_op jit(solution)/shard_map/reduce_scatter | solution.py:222
  390.3 1.4 divide_subtract_fusion.2
  391.7 76.9 %reduce-scatter.16.cloned.1.call-done = f32[3,3,16,128]{3,2,1,0:T(8,128)} async-done(((f32[3,3,256,128]{3,2,1,0:T(8,128)}), f32[3,3,16,128]{3,2,1,0:T(8,128)}) %reduce-scatter.16.cloned.1.call-update) | async-done | bytes 73744 | tf_op jit(solution)/shard_map/reduce_scatter | solution.py:221
  468.6 1.6 divide_subtract_fusion
  470.2 76.7 %reduce-scatter.12.cloned.1.call-done = f32[3,3,16,128]{3,2,1,0:T(8,128)} async-done(((f32[3,3,256,128]{3,2,1,0:T(8,128)}), f32[3,3,16,128]{3,2,1,0:T(8,128)}) %reduce-scatter.12.cloned.1.call-update) | async-done | bytes 73744 | tf_op jit(solution)/shard_map/reduce_scatter | solution.py:220
  546.9 1.6 divide_subtract_fusion.1
  (211 shorter events, 23.5 us)
Async XLA Ops:
  7.2 102.9 %copy-start = (bf16[2,19,19,256]{3,0,2,1:T(2,128)(2,1)S(1)}, bf16[2,19,19,256]{3,0,2,1:T(2,128)(2,1)}, u32[]{:S(2)}) copy-start(bf16[2,19,19,256]{3,0,2,1:T(2,128)(2,1)} %param.16) | copy-start | bytes 1108996
  7.2 56.9 %copy-start.39 = (u32[32]{0:T(128)S(1)}, u32[32]{0:T(128)}, u32[]{:S(2)}) copy-start(u32[32]{0:T(128)} %constant.145) | copy-start | bytes 388
  7.2 54.9 %copy-start.37 = (s32[2,2]{1,0:T(2,128)S(1)}, s32[2,2]{1,0:T(2,128)}, u32[]{:S(2)}) copy-start(s32[2,2]{1,0:T(2,128)} %param.17) | copy-start | bytes 52
  7.2 56.8 %copy-start.29 = (f32[1,16]{1,0:T(1,128)S(1)}, f32[1,16]{1,0:T(1,128)}, u32[]{:S(2)}) copy-start(f32[1,16]{1,0:T(1,128)} %param.23) | copy-start | bytes 196
  7.2 150.1 %all-gather.4.cloned.1.call-start = ((), (), s32[]{:S(2)}) async-start(), calls=%async_computation.8 | async-start | bytes 1769472 | tf_op jit(solution)/shard_map/all_gather | solution.py:132
  58.3 52.6 %copy-start.18 = (f32[1,16,601]{2,1,0:T(8,128)S(1)}, f32[1,16,601]{2,1,0:T(8,128)}, u32[]{:S(2)}) copy-start(f32[1,16,601]{2,1,0:T(8,128)} %param.22) | copy-start | bytes 115396
  58.3 97.0 %all-to-all-start = ((bf16[16,3,3,16,128]{4,3,2,1,0:T(8,128)(2,1)}), bf16[16,3,3,16,128]{4,3,2,1,0:T(8,128)(2,1)S(1)}, u32[]{:S(2)}, u32[]{:S(2)}) async-start(bf16[16,3,3,16,128]{4,3,2,1,0:T(8,128)(2,1)} %stack.203), calls=%async_computation | async-start | bytes 1179648 | tf_op jit(solution)/shard_map/all_to_all | solution.py:18
  62.0 86.3 %copy-start.32 = (s32[2,2]{1,0:T(2,128)S(1)}, s32[2,2]{1,0:T(2,128)}, u32[]{:S(2)}) copy-start(s32[2,2]{1,0:T(2,128)} %param.19) | copy-start | bytes 52
  62.1 86.3 %copy-start.33 = (s32[2,2]{1,0:T(2,128)S(1)}, s32[2,2]{1,0:T(2,128)}, u32[]{:S(2)}) copy-start(s32[2,2]{1,0:T(2,128)} %param.18) | copy-start | bytes 52
  62.1 101.2 %all-gather.6.cloned.1.call-start = ((), (), s32[]{:S(2)}) async-start(), calls=%async_computation.9 | async-start | bytes 1769472 | tf_op jit(solution)/shard_map/all_gather | solution.py:133
  110.9 46.4 %copy-start.27 = (pred[8,3]{0,1:T(4,128)(4,1)S(1)}, pred[8,3]{0,1:T(4,128)(4,1)}, u32[]{:S(2)}) copy-start(pred[8,3]{0,1:T(4,128)(4,1)} %constant.135) | copy-start | bytes 76
  156.3 70.4 %reduce-scatter.18.cloned.1.call-start = ((), (), s32[]{:S(2)}) async-start(), calls=%async_computation.14 | async-start | bytes 1966080 | tf_op jit(solution)/shard_map/reduce_scatter | solution.py:216
  159.3 0.8 copy-start.9
  167.4 0.7 copy-start.1
  168.4 3.0 copy-start.36
  170.5 0.9 copy-start.11
  175.5 3.3 copy-start.12
  178.8 2.8 copy-start.34
  180.9 0.7 copy-start.5
  186.3 2.3 copy-start.7
  188.7 38.7 %reduce-scatter.14.cloned.1.call-start = ((), (), s32[]{:S(2)}) async-start(), calls=%async_computation.12 | async-start | bytes 3538944 | tf_op jit(solution)/shard_map/reduce_scatter | solution.py:215
  188.9 2.7 copy-start.16
  197.9 2.5 copy-start.3
  201.5 2.2 copy-start.17
  204.0 0.9 copy-start.4
  208.5 0.9 copy-start.8
  208.5 1.1 copy-start.10
  208.5 1.2 copy-start.20
  208.5 3.1 copy-start.6
  208.5 3.8 copy-start.15
  208.5 24.7 %reduce-scatter.10.cloned.1.call-start = ((), (), s32[]{:S(2)}) async-start(), calls=%async_computation.10 | async-start | bytes 3538944 | tf_op jit(solution)/shard_map/reduce_scatter | solution.py:214
  214.4 0.9 copy-start.2
  219.7 0.7 copy-start.38
  219.7 1.4 copy-start.35
  219.7 93.7 %reduce-scatter.22.cloned.1.call-start = ((), (), s32[]{:S(2)}) async-start(), calls=%async_computation.16 | async-start | bytes 139264
  222.3 91.8 %copy-start.30 = (f32[1,16]{1,0:T(1,128)S(1)}, f32[1,16]{1,0:T(1,128)}, u32[]{:S(2)}) copy-start(f32[1,16]{1,0:T(1,128)} %param.30) | copy-start | bytes 196
  222.3 91.8 %copy-start.31 = (f32[1,16]{1,0:T(1,128)S(1)}, f32[1,16]{1,0:T(1,128)}, u32[]{:S(2)}) copy-start(f32[1,16]{1,0:T(1,128)} %param.31) | copy-start | bytes 196
  222.3 167.9 %copy-start.19 = (f32[1,16,601]{2,1,0:T(8,128)S(1)}, f32[1,16,601]{2,1,0:T(8,128)}, u32[]{:S(2)}) copy-start(f32[1,16,601]{2,1,0:T(8,128)} %param.22) | copy-start | bytes 115396
  222.4 167.9 %copy-start.25 = (f32[1,16,601]{2,1,0:T(8,128)S(1)}, f32[1,16,601]{2,1,0:T(8,128)}, u32[]{:S(2)}) copy-start(f32[1,16,601]{2,1,0:T(8,128)} %param.28) | copy-start | bytes 115396
  222.4 167.9 %copy-start.26 = (f32[1,16,601]{2,1,0:T(8,128)S(1)}, f32[1,16,601]{2,1,0:T(8,128)}, u32[]{:S(2)}) copy-start(f32[1,16,601]{2,1,0:T(8,128)} %param.29) | copy-start | bytes 115396
  222.4 246.2 %copy-start.13 = (f32[3,3,16,128]{3,2,1,0:T(8,128)S(1)}, f32[3,3,16,128]{3,2,1,0:T(8,128)}, u32[]{:S(2)}) copy-start(f32[3,3,16,128]{3,2,1,0:T(8,128)} %param.21) | copy-start | bytes 221188
  222.4 246.2 %copy-start.21 = (f32[3,3,16,128]{3,2,1,0:T(8,128)S(1)}, f32[3,3,16,128]{3,2,1,0:T(8,128)}, u32[]{:S(2)}) copy-start(f32[3,3,16,128]{3,2,1,0:T(8,128)} %param.26) | copy-start | bytes 221188
  222.4 246.2 %copy-start.22 = (f32[3,3,16,128]{3,2,1,0:T(8,128)S(1)}, f32[3,3,16,128]{3,2,1,0:T(8,128)}, u32[]{:S(2)}) copy-start(f32[3,3,16,128]{3,2,1,0:T(8,128)} %param.27) | copy-start | bytes 221188
  222.4 324.5 %copy-start.14 = (f32[3,3,16,128]{3,2,1,0:T(8,128)S(1)}, f32[3,3,16,128]{3,2,1,0:T(8,128)}, u32[]{:S(2)}) copy-start(f32[3,3,16,128]{3,2,1,0:T(8,128)} %param.20) | copy-start | bytes 221188
  222.4 324.5 %copy-start.23 = (f32[3,3,16,128]{3,2,1,0:T(8,128)S(1)}, f32[3,3,16,128]{3,2,1,0:T(8,128)}, u32[]{:S(2)}) copy-start(f32[3,3,16,128]{3,2,1,0:T(8,128)} %param.24) | copy-start | bytes 221188
  222.4 324.5 %copy-start.24 = (f32[3,3,16,128]{3,2,1,0:T(8,128)S(1)}, f32[3,3,16,128]{3,2,1,0:T(8,128)}, u32[]{:S(2)}) copy-start(f32[3,3,16,128]{3,2,1,0:T(8,128)} %param.25) | copy-start | bytes 221188
  226.6 163.7 %reduce-scatter.20.cloned.1.call-start = ((), (), s32[]{:S(2)}) async-start(), calls=%async_computation.15 | async-start | bytes 696320 | tf_op jit(solution)/shard_map/reduce_scatter | solution.py:222
  227.3 241.3 %reduce-scatter.16.cloned.1.call-start = ((), (), s32[]{:S(2)}) async-start(), calls=%async_computation.13 | async-start | bytes 1253376 | tf_op jit(solution)/shard_map/reduce_scatter | solution.py:221
  228.1 318.9 %reduce-scatter.12.cloned.1.call-start = ((), (), s32[]{:S(2)}) async-start(), calls=%async_computation.11 | async-start | bytes 1253376 | tf_op jit(solution)/shard_map/reduce_scatter | solution.py:220
  314.2 234.4 %copy-start.28 = (f32[1,16]{1,0:T(1,128)}, f32[1,16]{1,0:T(1,128)S(1)}, u32[]{:S(2)}) copy-start(f32[1,16]{1,0:T(1,128)S(1)} %copy.110) | copy-start | bytes 196
Sparse Core Ops, SparseCore 0:
  56.6 4.7 all-gather.3
  156.4 6.8 all-gather.5
  188.8 9.8 reduce-scatter.17
  208.6 11.1 reduce-scatter.13
  221.9 11.2 reduce-scatter.9
  235.3 78.0 reduce-scatter.21
  316.2 74.0 reduce-scatter.19
  393.1 75.4 reduce-scatter.15
  471.5 75.4 reduce-scatter.11
